TPU v7x, 128 devices: a whole 4x4x4 slice. The times are simulated.
128 devices in a mesh: row: 8 (over x_lo, z), col: 16 (over y, x_hi, core).
Axes of the slice: x: 4 (x_hi: 2, x_lo: 2; x = x_hi * 2 + x_lo), y: 4, z: 4, core: 2. Of those that a mesh axis runs over, the one named last changes fastest.
Arguments:
- q_base: bfloat16 [8192, 8192], P('row', 'col'), may hold values from -600 to 600
- q_down: bfloat16 [64, 8192], P(None, 'col'), may hold values from -1.1953125 to 1.1953125
- q_up: bfloat16 [8192, 64], P('row'), may hold values from -1.1953125 to 1.1953125
- q_magnitude: float32 [8192], P('row'), may hold values from 40 to 200
- k_base: bfloat16 [1024, 8192], P('row', 'col'), may hold values from -600 to 600
- k_down: bfloat16 [64, 8192], P(None, 'col'), may hold values from -1.1953125 to 1.1953125
- k_up: bfloat16 [1024, 64], P('row'), may hold values from -1.1953125 to 1.1953125
- k_magnitude: float32 [1024], P('row'), may hold values from 40 to 200
- v_base: bfloat16 [1024, 8192], P('row', 'col'), may hold values from -600 to 600
- v_down: bfloat16 [64, 8192], P(None, 'col'), may hold values from -1.1953125 to 1.1953125
- v_up: bfloat16 [1024, 64], P('row'), may hold values from -1.1953125 to 1.1953125
- v_magnitude: float32 [1024], P('row'), may hold values from 40 to 200
- o_base: bfloat16 [8192, 8192], P('row', 'col'), may hold values from -600 to 600
- o_down: bfloat16 [64, 8192], P(None, 'col'), may hold values from -1.1953125 to 1.1953125
- o_up: bfloat16 [8192, 64], P('row'), may hold values from -1.1953125 to 1.1953125
- o_magnitude: float32 [8192], P('row'), may hold values from 40 to 200
- gate_base: bfloat16 [29568, 8192], P('row', 'col'), may hold values from -600 to 600
- gate_down: bfloat16 [64, 8192], P(None, 'col'), may hold values from -1.1953125 to 1.1953125
- gate_up: bfloat16 [29568, 64], P('row'), may hold values from -1.1953125 to 1.1953125
- gate_magnitude: float32 [29568], P('row'), may hold values from 40 to 200
- lift_base: bfloat16 [29568, 8192], P('row', 'col'), may hold values from -600 to 600
- lift_down: bfloat16 [64, 8192], P(None, 'col'), may hold values from -1.1953125 to 1.1953125
- lift_up: bfloat16 [29568, 64], P('row'), may hold values from -1.1953125 to 1.1953125
- lift_magnitude: float32 [29568], P('row'), may hold values from 40 to 200
Outputs:
- q_merged: bfloat16 [8192, 8192], P(('row', 'col'))
- k_merged: bfloat16 [1024, 8192], P(('row', 'col'))
- v_merged: bfloat16 [1024, 8192], P(('row', 'col'))
- o_merged: bfloat16 [8192, 8192], P(None, ('col', 'row'))
- gate_merged: bfloat16 [29568, 8192], P(('row', 'col'))
- lift_merged: bfloat16 [29568, 8192], P(('row', 'col'))
All inputs are finite; a program needn't handle non-finite values.
Results may differ from a plain program's by a relative error of at most 0.001.
Values may be sent and summed in bfloat16 or wider, within the bound.
A program may use at most 128 MiB of HBM per device.

v0:
```python
import jax
import jax.numpy as jnp
from jax import lax
from jax.sharding import Mesh
from jax.sharding import PartitionSpec as P

COL = ("col_0", "col_1", "col_2")
ROW_COL = ("row", "col_0", "col_1", "col_2")
COL_ROW = ("col_0", "col_1", "col_2", "row")


eps = 1e-06


def over_axes(value, axes):
    for axis in axes:
        value = lax.psum(value, axis)
    return value


def tile_merge(base, down, up, magnitude):
    direction = base.astype(jnp.float32) + jnp.dot(up, down, preferred_element_type=jnp.float32)
    partial_sum = jnp.sum(direction * direction, axis=1)
    total = over_axes(partial_sum, COL)
    factor = magnitude * lax.rsqrt(total + eps)
    return (direction * factor[:, None]).astype(jnp.bfloat16)


def row_split(base, down, up, magnitude):
    merged = tile_merge(base, down, up, magnitude)
    return lax.all_to_all(merged, COL, split_axis=0, concat_axis=1, tiled=True)


def on_device(
    q_base,
    q_down,
    q_up,
    q_magnitude,
    k_base,
    k_down,
    k_up,
    k_magnitude,
    v_base,
    v_down,
    v_up,
    v_magnitude,
    o_base,
    o_down,
    o_up,
    o_magnitude,
    gate_base,
    gate_down,
    gate_up,
    gate_magnitude,
    lift_base,
    lift_down,
    lift_up,
    lift_magnitude,
):
    q_merged = row_split(q_base, q_down, q_up, q_magnitude)
    k_merged = row_split(k_base, k_down, k_up, k_magnitude)
    v_merged = row_split(v_base, v_down, v_up, v_magnitude)
    o_tile = tile_merge(o_base, o_down, o_up, o_magnitude)
    o_merged = lax.all_to_all(o_tile, "row", split_axis=1, concat_axis=0, tiled=True)
    gate_merged = row_split(gate_base, gate_down, gate_up, gate_magnitude)
    lift_merged = row_split(lift_base, lift_down, lift_up, lift_magnitude)
    return (q_merged, k_merged, v_merged, o_merged, gate_merged, lift_merged)


def solution(mesh):
    finer = Mesh(
        mesh.devices.reshape(mesh.shape["row"], 4, 2, 2), ("row", "col_0", "col_1", "col_2")
    )
    placed = (
        P("row", COL),
        P(None, COL),
        P("row", None),
        P("row"),
        P("row", COL),
        P(None, COL),
        P("row", None),
        P("row"),
        P("row", COL),
        P(None, COL),
        P("row", None),
        P("row"),
        P("row", COL),
        P(None, COL),
        P("row", None),
        P("row"),
        P("row", COL),
        P(None, COL),
        P("row", None),
        P("row"),
        P("row", COL),
        P(None, COL),
        P("row", None),
        P("row"),
    )
    return jax.shard_map(
        on_device,
        mesh=finer,
        in_specs=placed,
        out_specs=(
            P(ROW_COL, None),
            P(ROW_COL, None),
            P(ROW_COL, None),
            P(None, COL_ROW),
            P(ROW_COL, None),
            P(ROW_COL, None),
        ),
        check_vma=False,
    )
```

profile of v0, /device:TPU:1, one launch (start us, length us, event | category | flops | bytes accessed | tf_op | source)
XLA Modules:
  0.0 232.9 jit_solution(16911114155286947436)
XLA Ops:
  0.7 1.5 copy.39
  2.2 1.4 multiply_reduce_fusion.5
  3.6 1.3 multiply_reduce_fusion.4
  4.9 2.7 %multiply_reduce_fusion.2 = (f32[1024]{0:T(1024)S(1)}, f32[1024,512]{0,1:T(8,128)}) fusion(bf16[1024,64]{0,1:T(8,128)(2,1)} %param.38, bf16[64,512]{1,0:T(8,128)(2,1)} %param.37, bf16[1024,512]{0,1:T(8,128)(2,1)S(1)} %copy.39), kind=kOutput, calls=%fused_computation.7 | convolution fusion | flops 69204992 | bytes 3346432 | tf_op jit(solution)/shard_map/dot_general | solution.py:22
  7.6 1.8 multiply_reduce_fusion.3
  9.5 4.3 %multiply_reduce_fusion.1 = (f32[3696]{0:T(1024)S(1)}, f32[3696,512]{1,0:T(8,128)}) fusion(bf16[3696,64]{0,1:T(8,128)(2,1)S(1)} %copy-done, bf16[64,512]{1,0:T(8,128)(2,1)S(1)} %copy-done.6, bf16[3696,512]{1,0:T(8,128)(2,1)S(1)} %copy-done.2), kind=kOutput, calls=%fused_computation.4 | convolution fusion | flops 249786768 | bytes 11907520 | tf_op jit(solution)/shard_map/dot_general | solution.py:22
  13.8 4.4 %multiply_reduce_fusion = (f32[3696]{0:T(1024)S(1)}, f32[3696,512]{1,0:T(8,128)}) fusion(bf16[3696,64]{0,1:T(8,128)(2,1)S(1)} %copy-done.4, bf16[64,512]{1,0:T(8,128)(2,1)S(1)} %copy-done.7, bf16[3696,512]{1,0:T(8,128)(2,1)S(1)} %copy-done.3), kind=kOutput, calls=%fused_computation.1 | convolution fusion | flops 249786768 | bytes 11907520 | tf_op jit(solution)/shard_map/dot_general | solution.py:22
  18.2 14.8 %all-reduce = (f32[1024]{0:T(1024)S(1)}, f32[128]{0:T(128)S(1)}, f32[128]{0:T(128)S(1)}, f32[1024]{0:T(1024)S(1)}, f32[3696]{0:T(1024)S(1)}, /*index=5*/f32[3696]{0:T(1024)S(1)}) all-reduce(f32[1024]{0:T(1024)S(1)} %get-tuple-element.24, ...), channel_id=1, replica_groups=mesh['row'=8,'col_0'=4,'col_1'=2,'col_2'=2] {'col_0'}, use_global_device_ids=true, to_apply=%region_1.0 | all-reduce | flops 9696 | bytes 77568 | tf_op jit(solution)/shard_map/psum | solution.py:17
  33.0 9.6 %all-reduce.2 = (f32[1024]{0:T(1024)S(1)}, f32[128]{0:T(128)S(1)}, f32[128]{0:T(128)S(1)}, f32[1024]{0:T(1024)S(1)}, f32[3696]{0:T(1024)S(1)}, /*index=5*/f32[3696]{0:T(1024)S(1)}) all-reduce(f32[1024]{0:T(1024)S(1)} %get-tuple-element.6, ...), channel_id=1, replica_groups=mesh['row'=8,'col_0'=4,'col_1'=2,'col_2'=2] {'col_1'}, use_global_device_ids=true, to_apply=%region_2.0 | all-reduce | flops 9696 | bytes 77568 | tf_op jit(solution)/shard_map/psum | solution.py:17
  42.7 9.8 %all-reduce.1 = (f32[1024]{0:T(1024)S(1)}, f32[128]{0:T(128)S(1)}, f32[128]{0:T(128)S(1)}, f32[1024]{0:T(1024)S(1)}, f32[3696]{0:T(1024)S(1)}, /*index=5*/f32[3696]{0:T(1024)S(1)}) all-reduce(f32[1024]{0:T(1024)S(1)} %get-tuple-element.18, ...), channel_id=1, replica_groups=mesh['row'=8,'col_0'=4,'col_1'=2,'col_2'=2] {'col_2'}, use_global_device_ids=true, to_apply=%region_3.0 | all-reduce | flops 9696 | bytes 77568 | tf_op jit(solution)/shard_map/psum | solution.py:17
  53.2 3.5 %all-to-all-start.2 = ((bf16[16,8,512]{2,1,0:T(8,128)(2,1)}), bf16[16,8,512]{2,1,0:T(8,128)(2,1)S(1)}, u32[]{:S(2)}, u32[]{:S(2)}) async-start(bf16[16,8,512]{2,1,0:T(8,128)(2,1)} %fusion.1), calls=%async_computation.2 | async-start | bytes 262144 | tf_op jit(solution)/shard_map/all_to_all | solution.py:31
  57.5 6.9 %all-to-all-done.2 = bf16[16,8,512]{2,1,0:T(8,128)(2,1)S(1)} async-done(((bf16[16,8,512]{2,1,0:T(8,128)(2,1)}), bf16[16,8,512]{2,1,0:T(8,128)(2,1)S(1)}, u32[]{:S(2)}, u32[]{:S(2)}) %all-to-all-start.2) | async-done | bytes 131104 | tf_op jit(solution)/shard_map/all_to_all | solution.py:31
  64.4 4.0 %all-to-all-start.1 = ((bf16[16,8,512]{2,1,0:T(8,128)(2,1)}), bf16[16,8,512]{2,1,0:T(8,128)(2,1)S(1)}, u32[]{:S(2)}, u32[]{:S(2)}) async-start(bf16[16,8,512]{2,1,0:T(8,128)(2,1)} %fusion), calls=%async_computation.1 | async-start | bytes 262144 | tf_op jit(solution)/shard_map/all_to_all | solution.py:31
  68.4 2.8 %multiply_convert_fusion.2 = bf16[1024,512]{0,1:T(8,128)(2,1)} fusion(f32[1024,512]{0,1:T(8,128)} %get-tuple-element.31, f32[1024]{0:T(1024)S(1)} %get-tuple-element.38), kind=kLoop, calls=%fused_computation.6 | loop fusion | flops 1048576 | bytes 3149824 | tf_op jit(solution)/shard_map/convert_element_type | solution.py:26
  71.2 4.9 %all-to-all-done.1 = bf16[16,8,512]{2,1,0:T(8,128)(2,1)S(1)} async-done(((bf16[16,8,512]{2,1,0:T(8,128)(2,1)}), bf16[16,8,512]{2,1,0:T(8,128)(2,1)S(1)}, u32[]{:S(2)}, u32[]{:S(2)}) %all-to-all-start.1) | async-done | bytes 131104 | tf_op jit(solution)/shard_map/all_to_all | solution.py:31
  76.1 5.2 %all-to-all-start.3 = ((bf16[1024,8,64]{0,2,1:T(8,128)(2,1)}), bf16[1024,8,64]{0,2,1:T(8,128)(2,1)}, u32[]{:S(2)}, u32[]{:S(2)}) async-start(bf16[1024,8,64]{0,2,1:T(8,128)(2,1)} %bitcast.41), calls=%async_computation.3 | async-start | bytes 2097152 | tf_op jit(solution)/shard_map/all_to_all | solution.py:64
  82.5 14.0 %all-to-all-done.3 = bf16[1024,8,64]{0,2,1:T(8,128)(2,1)} async-done(((bf16[1024,8,64]{0,2,1:T(8,128)(2,1)}), bf16[1024,8,64]{0,2,1:T(8,128)(2,1)}, u32[]{:S(2)}, u32[]{:S(2)}) %all-to-all-start.3) | async-done | bytes 1048608 | tf_op jit(solution)/shard_map/all_to_all | solution.py:64
  96.5 4.1 %all-to-all-start = ((bf16[16,64,512]{2,1,0:T(8,128)(2,1)}), bf16[16,64,512]{2,1,0:T(8,128)(2,1)S(1)}, u32[]{:S(2)}, u32[]{:S(2)}) async-start(bf16[16,64,512]{2,1,0:T(8,128)(2,1)} %bitcast.42), calls=%async_computation | async-start | bytes 2097152 | tf_op jit(solution)/shard_map/all_to_all | solution.py:31
  100.7 5.3 %multiply_convert_fusion = bf16[3696,512]{1,0:T(8,128)(2,1)} fusion(f32[3696,512]{1,0:T(8,128)} %get-tuple-element.35, f32[3696]{0:T(1024)S(1)} %get-tuple-element.36), kind=kLoop, calls=%fused_computation | loop fusion | flops 3784704 | bytes 11368896 | tf_op jit(solution)/shard_map/convert_element_type | solution.py:26
  106.0 4.0 %all_to_all.104 = bf16[16,231,512]{2,1,0:T(8,128)(2,1)} reshape(bf16[3696,512]{1,0:T(8,128)(2,1)} %multiply_convert_fusion) | data formatting | bytes 7569408 | tf_op jit(solution)/shard_map/all_to_all | solution.py:31
  109.9 7.9 %all-to-all-done = bf16[16,64,512]{2,1,0:T(8,128)(2,1)S(1)} async-done(((bf16[16,64,512]{2,1,0:T(8,128)(2,1)}), bf16[16,64,512]{2,1,0:T(8,128)(2,1)S(1)}, u32[]{:S(2)}, u32[]{:S(2)}) %all-to-all-start) | async-done | bytes 1048608 | tf_op jit(solution)/shard_map/all_to_all | solution.py:31
  117.9 5.2 %all-to-all-start.5 = ((bf16[16,231,512]{2,1,0:T(8,128)(2,1)}), bf16[16,231,512]{2,1,0:T(8,128)(2,1)}, u32[]{:S(2)}, u32[]{:S(2)}) async-start(bf16[16,231,512]{2,1,0:T(8,128)(2,1)} %all_to_all.104), calls=%async_computation.5 | async-start | bytes 7602176 | tf_op jit(solution)/shard_map/all_to_all | solution.py:31
  123.1 5.3 %multiply_convert_fusion.1 = bf16[3696,512]{1,0:T(8,128)(2,1)} fusion(f32[3696,512]{1,0:T(8,128)} %get-tuple-element.33, f32[3696]{0:T(1024)S(1)} %get-tuple-element.37), kind=kLoop, calls=%fused_computation.3 | loop fusion | flops 3784704 | bytes 11368896 | tf_op jit(solution)/shard_map/convert_element_type | solution.py:26
  128.4 4.0 %all_to_all.100 = bf16[16,231,512]{2,1,0:T(8,128)(2,1)} reshape(bf16[3696,512]{1,0:T(8,128)(2,1)} %multiply_convert_fusion.1) | data formatting | bytes 7569408 | tf_op jit(solution)/shard_map/all_to_all | solution.py:31
  132.4 37.6 %all-to-all-done.5 = bf16[16,231,512]{2,1,0:T(8,128)(2,1)} async-done(((bf16[16,231,512]{2,1,0:T(8,128)(2,1)}), bf16[16,231,512]{2,1,0:T(8,128)(2,1)}, u32[]{:S(2)}, u32[]{:S(2)}) %all-to-all-start.5) | async-done | bytes 3784736 | tf_op jit(solution)/shard_map/all_to_all | solution.py:31
  169.9 5.3 %all-to-all-start.4 = ((bf16[16,231,512]{2,1,0:T(8,128)(2,1)}), bf16[16,231,512]{2,1,0:T(8,128)(2,1)}, u32[]{:S(2)}, u32[]{:S(2)}) async-start(bf16[16,231,512]{2,1,0:T(8,128)(2,1)} %all_to_all.100), calls=%async_computation.4 | async-start | bytes 7602176 | tf_op jit(solution)/shard_map/all_to_all | solution.py:31
  175.2 2.3 copy.44
  178.5 3.4 %copy.42 = bf16[231,16,512]{2,1,0:T(8,128)(2,1)S(1)} copy(bf16[231,16,512]{2,0,1:T(8,128)(2,1)} %bitcast.11) | data formatting | bytes 7569408 | tf_op jit(solution)/shard_map/all_to_all | solution.py:31
  182.3 5.8 %copy.46 = bf16[29,8,16,512]{3,1,2,0:T(8,128)(2,1)} copy(bf16[29,8,16,512]{3,2,1,0:T(8,128)(2,1)S(1)} %bitcast.39) | data formatting | bytes 7602176
  188.1 33.9 %all-to-all-done.4 = bf16[16,231,512]{2,1,0:T(8,128)(2,1)} async-done(((bf16[16,231,512]{2,1,0:T(8,128)(2,1)}), bf16[16,231,512]{2,1,0:T(8,128)(2,1)}, u32[]{:S(2)}, u32[]{:S(2)}) %all-to-all-start.4) | async-done | bytes 3784736 | tf_op jit(solution)/shard_map/all_to_all | solution.py:31
  222.0 3.4 %copy.41 = bf16[231,16,512]{2,1,0:T(8,128)(2,1)S(1)} copy(bf16[231,16,512]{2,0,1:T(8,128)(2,1)} %bitcast.10) | data formatting | bytes 7569408 | tf_op jit(solution)/shard_map/all_to_all | solution.py:31
  225.8 5.8 %copy.45 = bf16[29,8,16,512]{3,1,2,0:T(8,128)(2,1)} copy(bf16[29,8,16,512]{3,2,1,0:T(8,128)(2,1)S(1)} %bitcast.38) | data formatting | bytes 7602176
  (42 shorter events, 5.9 us)
Async XLA Ops:
  0.6 8.8 %copy-start = (bf16[3696,64]{0,1:T(8,128)(2,1)S(1)}, bf16[3696,64]{0,1:T(8,128)(2,1)}, u32[]{:S(2)}) copy-start(bf16[3696,64]{0,1:T(8,128)(2,1)} %param.42) | copy-start | bytes 1419268
  0.6 7.0 %copy-start.5 = (bf16[1024,64]{0,1:T(8,128)(2,1)S(1)}, bf16[1024,64]{0,1:T(8,128)(2,1)}, u32[]{:S(2)}) copy-start(bf16[1024,64]{0,1:T(8,128)(2,1)} %param.26) | copy-start | bytes 393220
  0.7 7.0 %copy-start.8 = (bf16[64,512]{1,0:T(8,128)(2,1)S(1)}, bf16[64,512]{1,0:T(8,128)(2,1)}, u32[]{:S(2)}) copy-start(bf16[64,512]{1,0:T(8,128)(2,1)} %param.25) | copy-start | bytes 196612
  2.2 7.2 %copy-start.2 = (bf16[3696,512]{1,0:T(8,128)(2,1)S(1)}, bf16[3696,512]{1,0:T(8,128)(2,1)}, u32[]{:S(2)}) copy-start(bf16[3696,512]{1,0:T(8,128)(2,1)} %param.40) | copy-start | bytes 11354116
  2.2 7.2 %copy-start.6 = (bf16[64,512]{1,0:T(8,128)(2,1)S(1)}, bf16[64,512]{1,0:T(8,128)(2,1)}, u32[]{:S(2)}) copy-start(bf16[64,512]{1,0:T(8,128)(2,1)} %param.41) | copy-start | bytes 196612
  9.4 4.3 %copy-start.3 = (bf16[3696,512]{1,0:T(8,128)(2,1)S(1)}, bf16[3696,512]{1,0:T(8,128)(2,1)}, u32[]{:S(2)}) copy-start(bf16[3696,512]{1,0:T(8,128)(2,1)} %param.44) | copy-start | bytes 11354116
  9.4 4.3 %copy-start.4 = (bf16[3696,64]{0,1:T(8,128)(2,1)S(1)}, bf16[3696,64]{0,1:T(8,128)(2,1)}, u32[]{:S(2)}) copy-start(bf16[3696,64]{0,1:T(8,128)(2,1)} %param.46) | copy-start | bytes 1419268
  9.5 4.3 %copy-start.7 = (bf16[64,512]{1,0:T(8,128)(2,1)S(1)}, bf16[64,512]{1,0:T(8,128)(2,1)}, u32[]{:S(2)}) copy-start(bf16[64,512]{1,0:T(8,128)(2,1)} %param.45) | copy-start | bytes 196612
  13.8 38.7 %copy-start.13 = (f32[128]{0:T(128)S(1)}, f32[128]{0:T(128)}, u32[]{:S(2)}) copy-start(f32[128]{0:T(128)} %param.35) | copy-start | bytes 1540
  13.8 42.9 %copy-start.14 = (f32[128]{0:T(128)S(1)}, f32[128]{0:T(128)}, u32[]{:S(2)}) copy-start(f32[128]{0:T(128)} %param.31) | copy-start | bytes 1540
  13.8 43.7 %copy-start.11 = (f32[1024]{0:T(1024)S(1)}, f32[1024]{0:T(1024)}, u32[]{:S(2)}) copy-start(f32[1024]{0:T(1024)} %param.39) | copy-start | bytes 12292
  13.8 43.7 %copy-start.12 = (f32[1024]{0:T(1024)S(1)}, f32[1024]{0:T(1024)}, u32[]{:S(2)}) copy-start(f32[1024]{0:T(1024)} %param.27) | copy-start | bytes 12292
  18.2 63.1 %copy-start.9 = (f32[3696]{0:T(1024)S(1)}, f32[3696]{0:T(1024)}, u32[]{:S(2)}) copy-start(f32[3696]{0:T(1024)} %param.47) | copy-start | bytes 44356
  18.2 63.1 %copy-start.10 = (f32[3696]{0:T(1024)S(1)}, f32[3696]{0:T(1024)}, u32[]{:S(2)}) copy-start(f32[3696]{0:T(1024)} %param.43) | copy-start | bytes 44356
  53.2 11.2 %all-to-all-start.2 = ((bf16[16,8,512]{2,1,0:T(8,128)(2,1)}), bf16[16,8,512]{2,1,0:T(8,128)(2,1)S(1)}, u32[]{:S(2)}, u32[]{:S(2)}) async-start(bf16[16,8,512]{2,1,0:T(8,128)(2,1)} %fusion.1), calls=%async_computation.2 | async-start | bytes 262144 | tf_op jit(solution)/shard_map/all_to_all | solution.py:31
  64.4 11.7 %all-to-all-start.1 = ((bf16[16,8,512]{2,1,0:T(8,128)(2,1)}), bf16[16,8,512]{2,1,0:T(8,128)(2,1)S(1)}, u32[]{:S(2)}, u32[]{:S(2)}) async-start(bf16[16,8,512]{2,1,0:T(8,128)(2,1)} %fusion), calls=%async_computation.1 | async-start | bytes 262144 | tf_op jit(solution)/shard_map/all_to_all | solution.py:31
  76.1 20.4 %all-to-all-start.3 = ((bf16[1024,8,64]{0,2,1:T(8,128)(2,1)}), bf16[1024,8,64]{0,2,1:T(8,128)(2,1)}, u32[]{:S(2)}, u32[]{:S(2)}) async-start(bf16[1024,8,64]{0,2,1:T(8,128)(2,1)} %bitcast.41), calls=%async_computation.3 | async-start | bytes 2097152 | tf_op jit(solution)/shard_map/all_to_all | solution.py:64
  96.5 21.3 %all-to-all-start = ((bf16[16,64,512]{2,1,0:T(8,128)(2,1)}), bf16[16,64,512]{2,1,0:T(8,128)(2,1)S(1)}, u32[]{:S(2)}, u32[]{:S(2)}) async-start(bf16[16,64,512]{2,1,0:T(8,128)(2,1)} %bitcast.42), calls=%async_computation | async-start | bytes 2097152 | tf_op jit(solution)/shard_map/all_to_all | solution.py:31
  117.9 52.0 %all-to-all-start.5 = ((bf16[16,231,512]{2,1,0:T(8,128)(2,1)}), bf16[16,231,512]{2,1,0:T(8,128)(2,1)}, u32[]{:S(2)}, u32[]{:S(2)}) async-start(bf16[16,231,512]{2,1,0:T(8,128)(2,1)} %all_to_all.104), calls=%async_computation.5 | async-start | bytes 7602176 | tf_op jit(solution)/shard_map/all_to_all | solution.py:31
  169.9 52.1 %all-to-all-start.4 = ((bf16[16,231,512]{2,1,0:T(8,128)(2,1)}), bf16[16,231,512]{2,1,0:T(8,128)(2,1)}, u32[]{:S(2)}, u32[]{:S(2)}) async-start(bf16[16,231,512]{2,1,0:T(8,128)(2,1)} %all_to_all.100), calls=%async_computation.4 | async-start | bytes 7602176 | tf_op jit(solution)/shard_map/all_to_all | solution.py:31
  225.8 7.1 %copy-start.1 = (bf16[3696,64]{0,1:T(8,128)(2,1)S(1)}, bf16[3696,64]{0,1:T(8,128)(2,1)}, u32[]{:S(2)}) copy-start(bf16[3696,64]{0,1:T(8,128)(2,1)} %param.42) | copy-start | bytes 1419268
where the time goes:
time: 234 us; the launch traced here: 233 us
  waiting for transfers between devices  105 us (45%)
  blocking collectives  34.2 us (15%)
  local copies, waits for them, and re-layouts  33.2 us (14%)
  starting transfers between devices  27.3 us (12%)
  other arithmetic  16.1 us (7%)
  matrix products  15.8 us (7%)
    all_to_all x5, waiting for transfers between devices, row_split(): return lax.all_to_all(merged, COL, split_axis=0, concat_axis=1, tiled=True)  91.2 us
    psum x3, blocking collectives, over_axes(): value = lax.psum(value, axis)  34.2 us
    all_to_all x5, starting transfers between devices, row_split(): return lax.all_to_all(merged, COL, split_axis=0, concat_axis=1, tiled=True)  22.2 us
    dot_general x6, matrix products, tile_merge(): jnp.dot(up, down, preferred_element_type=jnp.float32)  15.8 us
    all_to_all x5, local copies, waits for them, and re-layouts, row_split(): return lax.all_to_all(merged, COL, split_axis=0, concat_axis=1, tiled=True)  15.7 us
    unnamed x37, local copies, waits for them, and re-layouts  15.3 us
    convert_element_type x4, other arithmetic, tile_merge(): return (direction * factor[:, None]).astype(jnp.bfloat16)  14.6 us
    all_to_all x1, waiting for transfers between devices, on_device(): lax.all_to_all(o_tile, 'row', split_axis=1, concat_axis=0, tiled=True)  14 us
  transfers between devices with their start and end apart: 6, of which 6 were waited for; matrix products, arithmetic and copies ran while one was open for 12% of the time, Pallas kernels for 0%

commit v1 on v0

v1 whole, which is shorter than its diff:
```python
import jax
import jax.numpy as jnp
from jax import lax
from jax.experimental import pallas as pl
from jax.experimental.pallas import tpu as pltpu
from jax.sharding import PartitionSpec as P

MESH = pl.DeviceIdType.MESH
NAMES = ("q", "k", "v", "o", "gate", "lift")
ROW_SPLIT = ("k", "v", "q", "gate", "lift")
eps = 1e-06
LANES = 128


def up_to(value, unit):
    return -(-value // unit) * unit


class Plan:
    def __init__(self, mesh, bases, rank):
        self.rows_n = mesh.shape["row"]
        self.cols_n = mesh.shape["col"]
        self.rank = rank
        self.height = {p: b.shape[0] for p, b in bases.items()}
        self.width = bases["q"].shape[1]
        self.tiles = {p: -(-h // LANES) for p, h in self.height.items()}
        self.block = {p: self.height[p] // self.cols_n for p in ROW_SPLIT}
        self.held = {p: up_to(self.block[p], 8) for p in ROW_SPLIT}
        self.first = {}
        count = 0
        for p in ("o", "gate", "lift"):
            self.first[p] = count
            count += self.tiles[p]
        self.share = -(-count // self.cols_n)
        assert self.share <= 8


def column_sums(square):
    folded = square[:, :LANES]
    for at in range(LANES, square.shape[1], LANES):
        folded = folded + square[:, at : at + LANES]
    return jnp.sum(folded.T, axis=0, keepdims=True)


def kernel(plan, *refs):
    cols_n, rows_n = plan.cols_n, plan.rows_n
    width, rank = plan.width, plan.rank
    it = iter(refs)
    base = {p: None for p in NAMES}
    down, up, mag = dict(base), dict(base), dict(base)
    for p in NAMES:
        base[p], down[p], up[p], mag[p] = next(it), next(it), next(it), next(it)
    out = {p: next(it) for p in NAMES}
    stage, downs, ups, mags = {}, {}, {}, {}
    for p in NAMES:
        stage[p], downs[p], ups[p], mags[p] = next(it), next(it), next(it), next(it)
    wide = {p: next(it) for p in NAMES}
    send = {p: next(it) for p in NAMES}
    scale = next(it)
    spare = next(it)
    sums_kv, sums_q, parts, owned, totals = (next(it) for _ in range(5))
    load_sem, own_sem, send_sem, recv_sem = (next(it) for _ in range(4))

    me = lax.axis_index("col")
    my_row = lax.axis_index("row")

    order = ("k", "v", "q", "o", "gate", "lift")
    loads = {}
    for i, p in enumerate(order):
        loads[p] = [
            pltpu.make_async_copy(src[p], dst[p], load_sem.at[4 * i + j])
            for j, (src, dst) in enumerate(((base, stage), (down, downs), (up, ups), (mag, mags)))
        ]
        for copy in loads[p]:
            copy.start()

    barrier = pltpu.get_barrier_semaphore()
    for s in range(1, cols_n):
        pl.semaphore_signal(
            barrier, inc=1, device_id={"col": lax.rem(me + s, cols_n)}, device_id_type=MESH
        )
    for s in range(1, rows_n):
        pl.semaphore_signal(
            barrier, inc=1, device_id={"row": lax.rem(my_row + s, rows_n)}, device_id_type=MESH
        )

    def col_copy(kind, s, src, dst):
        return pltpu.make_async_remote_copy(
            src_ref=src,
            dst_ref=dst,
            send_sem=send_sem.at[kind, s],
            recv_sem=recv_sem.at[kind, s],
            device_id={"col": lax.rem(me + s, cols_n)},
            device_id_type=MESH,
        )

    def each(fn):
        def step(s, carry):
            fn(s)
            return carry

        lax.fori_loop(1, cols_n, step, 0)

    def product(p, at, size):
        return lax.dot_general(
            ups[p][:, pl.ds(at, size)],
            downs[p][...],
            (((0,), (0,)), ((), ())),
            preferred_element_type=jnp.float32,
        )

    def direction(p, at, size):
        return stage[p][pl.ds(at, size), :].astype(jnp.float32) + product(p, at, size)

    def first_pass(p, put):
        height = plan.height[p]
        full = height // LANES

        def tile(t, carry):
            at = pl.multiple_of(t * LANES, LANES)
            d = direction(p, at, LANES)
            wide[p][pl.ds(at, LANES), :] = d
            put(t, column_sums(d * d))
            return carry

        lax.fori_loop(0, full, tile, 0)
        rest = height - full * LANES
        if rest:
            at = full * LANES
            d = direction(p, at, rest)
            wide[p][pl.ds(at, rest), :] = d
            fill = jnp.zeros((LANES - rest, width), jnp.float32)
            wide[p][pl.ds(at + rest, LANES - rest), :] = fill
            square = jnp.concatenate([d * d, fill], axis=0)
            put(full, column_sums(square))

    def first_pass_o(put):
        def tile(t, carry):
            at = pl.multiple_of(t * LANES, LANES)
            d = direction("o", at, LANES).T
            wide["o"][:, pl.ds(at, LANES)] = d
            put(t, jnp.sum(d * d, axis=0, keepdims=True))
            return carry

        lax.fori_loop(0, plan.tiles["o"], tile, 0)

    def magnitudes(p, t):
        full = plan.height[p] // LANES
        if isinstance(t, int) and t == full:
            rest = plan.height[p] - full * LANES
            spare[...] = jnp.zeros_like(spare)
            spare[0:1, 0:rest] = mags[p][:, full * LANES :]
            return spare[0:1, :]
        return mags[p][:, pl.ds(pl.multiple_of(t * LANES, LANES), LANES)]

    def factors(p, t, total):
        return magnitudes(p, t) * lax.rsqrt(total + eps)

    def fill_scale(p, total_of):
        def one(t):
            row = factors(p, t, total_of(t))
            at = t * LANES if isinstance(t, int) else pl.multiple_of(t * LANES, LANES)
            scale[pl.ds(at, LANES), :] = jnp.broadcast_to(row, (LANES, LANES)).T

        full = plan.height[p] // LANES

        def tile(t, carry):
            one(t)
            return carry

        lax.fori_loop(0, full, tile, 0)
        if plan.tiles[p] > full:
            one(full)

    def merged(p, at, size):
        factor = scale[pl.ds(at, size), :]
        return jnp.concatenate(
            [
                (wide[p][pl.ds(at, size), c : c + LANES] * factor).astype(jnp.bfloat16)
                for c in range(0, width, LANES)
            ],
            axis=1,
        )

    def block_copy(p, kind, s):
        target = lax.rem(me + s, cols_n)
        return col_copy(
            kind,
            s,
            send[p].at[target],
            out[p].at[:, pl.ds(pl.multiple_of(me * width, width), width)],
        )

    own = []

    def own_block(p, src, dst):
        copy = pltpu.make_async_copy(src, dst, own_sem.at[NAMES.index(p)])
        copy.start()
        own.append(copy)

    def own_rows(p):
        own_block(
            p, send[p].at[me], out[p].at[:, pl.ds(pl.multiple_of(me * width, width), width)]
        )

    KIND = {p: i for i, p in enumerate(ROW_SPLIT)}
    KV, Q, RS, AG = (len(ROW_SPLIT) + i for i in range(4))

    def tally(kind, buffer, wait_copy):
        each(lambda s: wait_copy(s).wait_recv())
        total = buffer[0]
        for c in range(1, cols_n):
            total = total + buffer[c]
        return total

    for p in ("k", "v"):
        for copy in loads[p]:
            copy.wait()
    sums_kv[me] = jnp.zeros(sums_kv.shape[1:], jnp.float32)
    for i, p in enumerate(("k", "v")):

        def put(t, sums, i=i):
            sums_kv[pl.ds(me, 1), i, :] = sums

        first_pass(p, put)

    pl.semaphore_wait(barrier, cols_n + rows_n - 2)

    def kv_copy(s):
        return col_copy(KV, s, sums_kv.at[me], sums_kv.at[me])

    each(lambda s: kv_copy(s).start())

    for copy in loads["q"]:
        copy.wait()

    def put_q(t, sums):
        sums_q[pl.ds(me, 1), pl.ds(t, 1), :] = sums.reshape(1, 1, LANES)

    first_pass("q", put_q)

    def q_copy(s):
        return col_copy(Q, s, sums_q.at[me], sums_q.at[me])

    each(lambda s: q_copy(s).start())

    parts[...] = jnp.zeros_like(parts)

    def put_later(p):
        def put(t, sums):
            slot = plan.first[p] + t
            owner, at = slot // plan.share, slot % plan.share
            parts[pl.ds(owner, 1), pl.ds(at, 1), :] = sums.reshape(1, 1, LANES)

        return put

    for copy in loads["o"]:
        copy.wait()
    first_pass_o(put_later("o"))

    total = tally(KV, sums_kv, kv_copy)
    for i, p in enumerate(("k", "v")):
        fill_scale(p, lambda t, i=i: total[i : i + 1, :])
        block = plan.block[p]
        for c in range(cols_n):
            send[p][c] = merged(p, c * block, block)
        each(lambda s, p=p: block_copy(p, KIND[p], s).start())
        own_rows(p)

    totals_q = tally(Q, sums_q, q_copy)
    spare[...] = totals_q
    fill_scale("q", lambda t: spare[pl.ds(t, 1), :])
    block = plan.block["q"]

    def q_block(c, carry):
        send["q"][c] = merged("q", pl.multiple_of(c * block, block), block)
        return carry

    lax.fori_loop(0, cols_n, q_block, 0)
    each(lambda s: block_copy("q", KIND["q"], s).start())
    own_rows("q")

    for p in ("gate", "lift"):
        for copy in loads[p]:
            copy.wait()
        first_pass(p, put_later(p))

    def rs_copy(s):
        target = lax.rem(me + s, cols_n)
        return col_copy(RS, s, parts.at[target], owned.at[me])

    each(lambda s: rs_copy(s).start())
    owned[me] = parts[me]
    totals[me] = tally(RS, owned, rs_copy)

    def ag_copy(s):
        return col_copy(AG, s, totals.at[me], totals.at[me])

    each(lambda s: ag_copy(s).start())
    each(lambda s: ag_copy(s).wait_recv())

    def later_total(p):
        def of(t):
            slot = plan.first[p] + t
            owner, at = slot // plan.share, slot % plan.share
            return totals[pl.ds(owner, 1), pl.ds(at, 1), :].reshape(1, LANES)

        return of

    total_of_o = later_total("o")

    def o_tile(t, carry):
        at = pl.multiple_of(t * LANES, LANES)
        factor = factors("o", t, total_of_o(t))
        send["o"][:, pl.ds(at, LANES)] = (wide["o"][:, pl.ds(at, LANES)] * factor).astype(
            jnp.bfloat16
        )
        return carry

    lax.fori_loop(0, plan.tiles["o"], o_tile, 0)
    depth = width // rows_n
    height = plan.height["o"]
    O = AG + 1
    o_place = out["o"].at[:, pl.ds(pl.multiple_of(my_row * height, height), height)]

    def o_copy(s):
        target = lax.rem(my_row + s, rows_n)
        return pltpu.make_async_remote_copy(
            src_ref=send["o"].at[pl.ds(pl.multiple_of(target * depth, depth), depth), :],
            dst_ref=o_place,
            send_sem=send_sem.at[O, s],
            recv_sem=recv_sem.at[O, s],
            device_id={"row": target},
            device_id_type=MESH,
        )

    for s in range(1, rows_n):
        o_copy(s).start()
    own_block("o", send["o"].at[pl.ds(pl.multiple_of(my_row * depth, depth), depth), :], o_place)

    for p in ("gate", "lift"):
        fill_scale(p, later_total(p))
        block, held = plan.block[p], plan.held[p]
        window = up_to(block + 15, 128)
        ahead = lax.broadcasted_iota(jnp.int32, (held, window), 1) - lax.broadcasted_iota(
            jnp.int32, (held, window), 0
        )

        def make(target, p=p, block=block, window=window, ahead=ahead):
            start = target * block
            at = pl.multiple_of(start // 16 * 16, 16)
            pick = jnp.where(ahead == start - at, 1.0, 0.0).astype(jnp.bfloat16)
            rows = merged(p, at, window)
            send[p][target] = jnp.dot(pick, rows, preferred_element_type=jnp.float32).astype(
                jnp.bfloat16
            )

        def go(s, p=p, make=make):
            make(lax.rem(me + s, cols_n))
            block_copy(p, KIND[p], s).start()

        each(go)
        make(me)
        own_rows(p)

    each(lambda s: kv_copy(s).wait_send())
    each(lambda s: q_copy(s).wait_send())
    each(lambda s: rs_copy(s).wait_send())
    each(lambda s: ag_copy(s).wait_send())
    for p in ROW_SPLIT:
        each(lambda s, p=p: block_copy(p, KIND[p], s).wait())
    for s in range(1, rows_n):
        o_copy(s).wait()
    for copy in own:
        copy.wait()


def solution(mesh):
    def on_device(*args):
        bases = {p: args[4 * i] for i, p in enumerate(NAMES)}
        rank = args[1].shape[0]
        plan = Plan(mesh, bases, rank)
        width, cols_n = plan.width, plan.cols_n
        bf16, f32 = jnp.bfloat16, jnp.float32
        operands, scratch = [], []
        for i, p in enumerate(NAMES):
            base, down, up, magnitude = args[4 * i : 4 * i + 4]
            operands += [base, down, up.T, magnitude.reshape(1, -1)]
            scratch += [
                pltpu.VMEM(base.shape, bf16),
                pltpu.VMEM(down.shape, bf16),
                pltpu.VMEM((rank, base.shape[0]), bf16),
                pltpu.VMEM((1, base.shape[0]), f32),
            ]
        shapes = []
        for p in NAMES:
            if p == "o":
                shapes.append((width // plan.rows_n, plan.height[p] * plan.rows_n))
                scratch.append(pltpu.VMEM((width, plan.height[p]), f32))
            else:
                shapes.append((plan.held[p], width * cols_n))
                scratch.append(pltpu.VMEM((plan.tiles[p] * LANES, width), f32))
        for p in NAMES:
            if p == "o":
                scratch.append(pltpu.VMEM((width, plan.height[p]), bf16))
            else:
                scratch.append(pltpu.VMEM((cols_n, plan.held[p], width), bf16))
        scratch.append(pltpu.VMEM((max(plan.tiles.values()) * LANES, LANES), f32))
        scratch.append(pltpu.VMEM((8, LANES), f32))
        scratch += [pltpu.VMEM((cols_n, 8, LANES), f32)] * 5
        scratch += [
            pltpu.SemaphoreType.DMA((24,)),
            pltpu.SemaphoreType.DMA((6,)),
            pltpu.SemaphoreType.DMA((10, cols_n)),
            pltpu.SemaphoreType.DMA((10, cols_n)),
        ]
        got = pl.pallas_call(
            lambda *refs: kernel(plan, *refs),
            out_shape=[jax.ShapeDtypeStruct(s, bf16) for s in shapes],
            in_specs=[pl.BlockSpec(memory_space=pl.ANY)] * len(operands),
            out_specs=[pl.BlockSpec(memory_space=pl.ANY)] * len(shapes),
            scratch_shapes=scratch,
            name="merge",
            compiler_params=pltpu.CompilerParams(
                collective_id=0, has_side_effects=True, vmem_limit_bytes=62 * 1024 * 1024
            ),
        )(*operands)
        outs = []
        for p, o in zip(NAMES, got):
            outs.append(o.T if p == "o" else o[: plan.block[p]])
        return tuple(outs)

    specs = []
    for p in NAMES:
        specs += [P("row", "col"), P(None, "col"), P("row", None), P("row")]
    by_row = P(("row", "col"), None)
    return jax.shard_map(
        on_device,
        mesh=mesh,
        in_specs=tuple(specs),
        out_specs=(by_row, by_row, by_row, P(None, ("col", "row")), by_row, by_row),
        check_vma=False,
    )
```

time: 234 us -> 160 us (0.68)
  Pallas kernels: 0 us -> 142 us
  waiting for transfers between devices: 105 us -> 0 us
  blocking collectives: 34.2 us -> 0 us
  starting transfers between devices: 27.3 us -> 0 us
  local copies, waits for them, and re-layouts: 33.2 us -> 15.8 us
  other arithmetic: 16.1 us -> 0 us
  matrix products: 15.8 us -> 0 us
    pallas_call x0 -> x1, Pallas kernels: none -> 142 us  [on_device(): pl.pallas_call(lambda *refs: kernel(plan, *refs), out_shape=[jax.ShapeDty...]
    all_to_all x6 -> x0, waiting for transfers between devices: 105 us -> none  [the longest x5 91.2 us: row_split(): return lax.all_to_all(merged, COL, split_axis=0, concat_axis=1, tiled=True)]
    psum x3 -> x0, blocking collectives: 34.2 us -> none  [over_axes(): value = lax.psum(value, axis)]
    all_to_all x6 -> x0, starting transfers between devices: 27.3 us -> none  [the longest x5 22.2 us: row_split(): return lax.all_to_all(merged, COL, split_axis=0, concat_axis=1, tiled=True)]
    all_to_all x6 -> x0, local copies, waits for them, and re-layouts: 18 us -> none  [the longest x5 15.7 us: row_split(): return lax.all_to_all(merged, COL, split_axis=0, concat_axis=1, tiled=True)]
    dot_general x6 -> x0, matrix products: 15.8 us -> none  [tile_merge(): jnp.dot(up, down, preferred_element_type=jnp.float32)]
    convert_element_type x4 -> x0, other arithmetic: 14.6 us -> none  [tile_merge(): return (direction * factor[:, None]).astype(jnp.bfloat16)]
    reshape x0 -> x2, local copies, waits for them, and re-layouts: none -> 2.66 us  [on_device(): operands += [base, down, up.T, magnitude.reshape(1, -1)]]
  transfers between devices with their start and end apart: 6 -> 0, of which waited for: 6 -> 0; matrix products, arithmetic and copies ran while one was open for 12% -> 0% of each run, Pallas kernels for 0% -> 0%
where the time goes in v1:
time: 160 us; the launch traced here: 158 us
  Pallas kernels  142 us (89%)
  local copies, waits for them, and re-layouts  15.8 us (10%)
    pallas_call x1, Pallas kernels, on_device(): pl.pallas_call(lambda *refs: kernel(plan, *refs), out_shape=[jax.ShapeDty...  142 us
    unnamed x10, local copies, waits for them, and re-layouts  13.1 us

profile of v1, /device:TPU:1, one launch (start us, length us, event | category | flops | bytes accessed | tf_op | source)
XLA Modules:
  0.0 158.3 jit_solution(16283855282265954996)
XLA Ops:
  0.6 1.3 reshape.34.refs_19_
  2.0 1.3 reshape.35.refs_23_
  3.3 141.9 %merge.1 = (bf16[64,8192]{1,0:T(8,128)(2,1)}, bf16[8,8192]{1,0:T(8,128)(2,1)}, bf16[8,8192]{1,0:T(8,128)(2,1)}, bf16[64,8192]{1,0:T(8,128)(2,1)}, bf16[232,8192]{1,0:T(8,128)(2,1)}, /*index=5*/bf16[232,8192]{1,0:T(8,128)(2,1)}) custom-call(bf16[1024,512]{1,0:T(8,128)(2,1)} %refs_0_.1, bf16[64,512]{1,0:T(8,128)(2,1)} %refs_1_.1, bf16[64,1024]{1,0:T(8,128)(2,1)} %bitcast.18, ...), custom_call_target="tpu_custom_call" | custom-call | tf_op jit(solution)/shard_map/merge/pallas_call | solution.py:417
  145.2 0.0 copy-start.1
  145.2 2.4 %copy.36 = bf16[64,8192]{1,0:T(8,128)(2,1)} copy(bf16[64,8192]{1,0:T(8,128)(2,1)} %get-tuple-element.24) | data formatting | bytes 2097152
  147.6 1.6 copy.37
  149.2 1.6 copy.38
  150.7 2.3 %copy.39 = bf16[8192,64]{0,1:T(8,128)(2,1)} copy(bf16[8192,64]{0,1:T(8,128)(2,1)} %bitcast.15) | data formatting | bytes 2097152
  153.0 0.0 copy-done.1
  153.0 0.0 copy-start
  153.0 1.9 %copy.40 = bf16[231,8192]{1,0:T(8,128)(2,1)} copy(bf16[231,8192]{1,0:T(8,128)(2,1)S(1)} %bitcast.14) | data formatting | bytes 7569408
  154.9 1.5 copy-done
  156.4 1.9 %copy.41 = bf16[231,8192]{1,0:T(8,128)(2,1)} copy(bf16[231,8192]{1,0:T(8,128)(2,1)S(1)} %bitcast.13) | data formatting | bytes 7569408
Async XLA Ops:
  145.2 7.8 %copy-start.1 = (bf16[232,8192]{1,0:T(8,128)(2,1)S(1)}, bf16[232,8192]{1,0:T(8,128)(2,1)}, u32[]{:S(2)}) copy-start(bf16[232,8192]{1,0:T(8,128)(2,1)} %get-tuple-element.16) | copy-start | bytes 11403268
  153.0 3.4 %copy-start = (bf16[232,8192]{1,0:T(8,128)(2,1)S(1)}, bf16[232,8192]{1,0:T(8,128)(2,1)}, u32[]{:S(2)}) copy-start(bf16[232,8192]{1,0:T(8,128)(2,1)} %get-tuple-element.17) | copy-start | bytes 11403268

commit v2 on v1

v2 whole, which is shorter than its diff:
```python
import jax
import jax.numpy as jnp
from jax import lax
from jax.experimental import pallas as pl
from jax.experimental.pallas import tpu as pltpu
from jax.sharding import PartitionSpec as P

MESH = pl.DeviceIdType.MESH
NAMES = ("q", "k", "v", "o", "gate", "lift")
ROW_SPLIT = ("k", "v", "q", "gate", "lift")
LATE = {"first": ("gate", "o"), "second": ("lift",)}
UNROLL = 4
eps = 1e-06
LANES = 128


def up_to(value, unit):
    return -(-value // unit) * unit


class Plan:
    def __init__(self, mesh, bases, rank):
        self.rows_n = mesh.shape["row"]
        self.cols_n = mesh.shape["col"]
        self.rank = rank
        self.height = {p: b.shape[0] for p, b in bases.items()}
        self.width = bases["q"].shape[1]
        self.tiles = {p: -(-h // LANES) for p, h in self.height.items()}
        self.block = {p: self.height[p] // self.cols_n for p in ROW_SPLIT}
        self.held = {p: up_to(self.block[p], 8) for p in ROW_SPLIT}
        self.begin, self.share = {}, {}
        for group, members in LATE.items():
            count = 0
            for p in members:
                self.begin[p] = (group, count)
                count += self.tiles[p]
            self.share[group] = -(-count // self.cols_n)
        self.early = {"k": 0, "v": self.tiles["k"], "q": self.tiles["k"] + self.tiles["v"]}
        self.early_rows = self.early["q"] + self.tiles["q"]


def loop(n, fn, unroll):
    trips = n // unroll

    def trip(g, carry):
        for u in range(unroll):
            fn(g * unroll + u)
        return carry

    if trips:
        lax.fori_loop(0, trips, trip, 0)
    for t in range(trips * unroll, n):
        fn(t)


def rows_at(t):
    return t * LANES if isinstance(t, int) else pl.multiple_of(t * LANES, LANES)


def column_sums(square):
    folded = square[:, :LANES]
    for at in range(LANES, square.shape[1], LANES):
        folded = folded + square[:, at : at + LANES]
    return jnp.sum(folded.T, axis=0, keepdims=True)


def kernel(plan, *refs):
    cols_n, rows_n = plan.cols_n, plan.rows_n
    width, rank = plan.width, plan.rank
    it = iter(refs)
    base = {p: None for p in NAMES}
    down, up, mag = dict(base), dict(base), dict(base)
    for p in NAMES:
        base[p], down[p], up[p], mag[p] = next(it), next(it), next(it), next(it)
    out = {p: next(it) for p in NAMES}
    stage, downs, ups, mags = {}, {}, {}, {}
    for p in NAMES:
        stage[p], downs[p], ups[p], mags[p] = next(it), next(it), next(it), next(it)
    wide = {p: next(it) for p in NAMES}
    send = {p: next(it) for p in NAMES}
    scale = next(it)
    spare = next(it)
    sums_early = next(it)
    parts = {p: next(it) for p in LATE}
    owned = {p: next(it) for p in LATE}
    totals = {p: next(it) for p in LATE}
    early_total = next(it)
    load_sem, own_sem, send_sem, recv_sem = (next(it) for _ in range(4))

    me = lax.axis_index("col")
    my_row = lax.axis_index("row")

    order = ("k", "v", "q", "o", "gate", "lift")
    loads = {}
    for i, p in enumerate(order):
        loads[p] = [
            pltpu.make_async_copy(src[p], dst[p], load_sem.at[4 * i + j])
            for j, (src, dst) in enumerate(((base, stage), (down, downs), (up, ups), (mag, mags)))
        ]

    def fetch(*names):
        for p in names:
            for copy in loads[p]:
                copy.start()

    fetch("k", "v", "q")

    barrier = pltpu.get_barrier_semaphore()
    for s in range(1, cols_n):
        pl.semaphore_signal(
            barrier, inc=1, device_id={"col": lax.rem(me + s, cols_n)}, device_id_type=MESH
        )
    for s in range(1, rows_n):
        pl.semaphore_signal(
            barrier, inc=1, device_id={"row": lax.rem(my_row + s, rows_n)}, device_id_type=MESH
        )

    def col_copy(kind, s, src, dst):
        return pltpu.make_async_remote_copy(
            src_ref=src,
            dst_ref=dst,
            send_sem=send_sem.at[kind, s],
            recv_sem=recv_sem.at[kind, s],
            device_id={"col": lax.rem(me + s, cols_n)},
            device_id_type=MESH,
        )

    def each(fn):
        def step(s, carry):
            fn(s)
            return carry

        lax.fori_loop(1, cols_n, step, 0)

    def direction(p, at, size):
        return stage[p][pl.ds(at, size), :].astype(jnp.float32) + lax.dot_general(
            ups[p][:, pl.ds(at, size)],
            downs[p][...],
            (((0,), (0,)), ((), ())),
            preferred_element_type=jnp.float32,
        )

    def first_pass(p, put, start, stop):
        height = plan.height[p]
        full = height // LANES

        def tile(t):
            at = rows_at(t)
            d = direction(p, at, LANES)
            wide[p][pl.ds(at, LANES), :] = d
            put(t, column_sums(d * d))

        loop(min(stop, full) - start, lambda t: tile(t + start), UNROLL)
        if stop > full:
            rest = height - full * LANES
            at = full * LANES
            d = direction(p, at, rest)
            wide[p][pl.ds(at, rest), :] = d
            fill = jnp.zeros((LANES - rest, width), jnp.float32)
            wide[p][pl.ds(at + rest, LANES - rest), :] = fill
            square = jnp.concatenate([d * d, fill], axis=0)
            put(full, column_sums(square))

    def magnitudes(p, t):
        full = plan.height[p] // LANES
        if isinstance(t, int) and t == full:
            rest = plan.height[p] - full * LANES
            spare[...] = jnp.zeros_like(spare)
            spare[0:1, 0:rest] = mags[p][full * LANES :].reshape(1, rest)
            return spare[0:1, :]
        return mags[p][pl.ds(rows_at(t), LANES)].reshape(1, LANES)

    def factors(p, t, total):
        return magnitudes(p, t) * lax.rsqrt(total + eps)

    def fill_scale(p, total_of):
        def one(t):
            row = factors(p, t, total_of(t))
            scale[pl.ds(rows_at(t), LANES), :] = jnp.broadcast_to(row, (LANES, LANES)).T

        full = plan.height[p] // LANES
        loop(full, one, UNROLL)
        if plan.tiles[p] > full:
            one(full)

    def merged(p, at, size):
        factor = scale[pl.ds(at, size), :]
        return jnp.concatenate(
            [
                (wide[p][pl.ds(at, size), c : c + LANES] * factor).astype(jnp.bfloat16)
                for c in range(0, width, LANES)
            ],
            axis=1,
        )

    KIND = {p: i for i, p in enumerate(ROW_SPLIT)}
    EARLY, O = len(ROW_SPLIT), len(ROW_SPLIT) + 1
    RS = {group: O + 1 + i for i, group in enumerate(LATE)}
    AG = {group: O + 3 + i for i, group in enumerate(LATE)}

    def block_copy(p, s):
        target = lax.rem(me + s, cols_n)
        return col_copy(
            KIND[p],
            s,
            send[p].at[target],
            out[p].at[:, pl.ds(pl.multiple_of(me * width, width), width)],
        )

    own = []

    def own_block(p, src, dst):
        copy = pltpu.make_async_copy(src, dst, own_sem.at[NAMES.index(p)])
        copy.start()
        own.append(copy)

    def own_rows(p):
        own_block(
            p, send[p].at[me], out[p].at[:, pl.ds(pl.multiple_of(me * width, width), width)]
        )

    def added(buffer):
        total = buffer[0]
        for c in range(1, cols_n):
            total = total + buffer[c]
        return total

    def arrive(p):
        for copy in loads[p]:
            copy.wait()

    def early_copy(s):
        return col_copy(EARLY, s, sums_early.at[me], sums_early.at[me])

    def put_early(p):
        def put(t, sums):
            sums_early[pl.ds(me, 1), pl.ds(plan.early[p] + t, 1), :] = sums.reshape(1, 1, LANES)

        return put

    for p in ("k", "v", "q"):
        arrive(p)
    fetch("gate", "o", "lift")
    for p in ("k", "v", "q"):
        first_pass(p, put_early(p), 0, plan.tiles[p])
    pl.semaphore_wait(barrier, cols_n + rows_n - 2)
    each(lambda s: early_copy(s).start())

    def place(p, t):
        group, begin = plan.begin[p]
        share = plan.share[group]
        return group, (begin + t) // share, (begin + t) % share

    def put_late(p):
        def put(t, sums):
            group, owner, at = place(p, t)
            parts[group][pl.ds(owner, 1), pl.ds(at, 1), :] = sums.reshape(1, 1, LANES)

        return put

    def late_total(p):
        def of(t):
            group, owner, at = place(p, t)
            return totals[group][pl.ds(owner, 1), pl.ds(at, 1), :].reshape(1, LANES)

        return of

    def rs_copy(group, s):
        target = lax.rem(me + s, cols_n)
        return col_copy(RS[group], s, parts[group].at[target], owned[group].at[me])

    def ag_copy(group, s):
        return col_copy(AG[group], s, totals[group].at[me], totals[group].at[me])

    def scatter(group):
        each(lambda s: rs_copy(group, s).start())
        owned[group][me] = parts[group][me]

    def gather(group):
        each(lambda s: rs_copy(group, s).wait_recv())
        totals[group][me] = added(owned[group])
        each(lambda s: ag_copy(group, s).start())

    def told(group):
        each(lambda s: ag_copy(group, s).wait_recv())

    def o_first(t):
        at = rows_at(t)
        d = direction("o", at, LANES).T
        wide["o"][:, pl.ds(at, LANES)] = d
        put_late("o")(t, jnp.sum(d * d, axis=0, keepdims=True))

    for group in LATE:
        parts[group][...] = jnp.zeros_like(parts[group])
    arrive("gate")
    first_pass("gate", put_late("gate"), 0, plan.tiles["gate"])
    arrive("o")
    loop(plan.tiles["o"], o_first, UNROLL)
    scatter("first")
    arrive("lift")
    first_pass("lift", put_late("lift"), 0, plan.tiles["lift"])
    scatter("second")

    each(lambda s: early_copy(s).wait_recv())
    early_total[...] = added(sums_early)

    def early_out(p):
        fill_scale(p, lambda t: early_total[pl.ds(plan.early[p] + t, 1), :])
        block = plan.block[p]

        def cut(c):
            at = c * block if isinstance(c, int) else pl.multiple_of(c * block, block)
            send[p][c] = merged(p, at, block)

        loop(cols_n, cut, UNROLL)
        each(lambda s: block_copy(p, s).start())
        own_rows(p)

    early_out("k")
    early_out("v")
    gather("first")
    early_out("q")
    gather("second")

    def make(p, target):
        block, held = plan.block[p], plan.held[p]
        window = up_to(block + 15, LANES)
        start = target * block
        at = pl.multiple_of(start // 16 * 16, 16)
        ahead = lax.broadcasted_iota(jnp.int32, (held, window), 1) - lax.broadcasted_iota(
            jnp.int32, (held, window), 0
        )
        pick = jnp.where(ahead == start - at, 1.0, 0.0).astype(jnp.bfloat16)
        rows = merged(p, at, window)
        send[p][target] = jnp.dot(pick, rows, preferred_element_type=jnp.float32).astype(
            jnp.bfloat16
        )

    def shifted_out(p):
        fill_scale(p, late_total(p))

        def one(s):
            make(p, lax.rem(me + s, cols_n))
            block_copy(p, s).start()

        each(one)
        make(p, me)
        own_rows(p)

    told("first")
    shifted_out("gate")

    def o_tile(t):
        at = rows_at(t)
        factor = factors("o", t, late_total("o")(t))
        send["o"][:, pl.ds(at, LANES)] = (wide["o"][:, pl.ds(at, LANES)] * factor).astype(
            jnp.bfloat16
        )

    loop(plan.tiles["o"], o_tile, UNROLL)
    depth = width // rows_n
    height = plan.height["o"]
    o_place = out["o"].at[:, pl.ds(pl.multiple_of(my_row * height, height), height)]

    def o_part(target):
        return send["o"].at[pl.ds(pl.multiple_of(target * depth, depth), depth), :]

    def o_copy(s):
        target = lax.rem(my_row + s, rows_n)
        return pltpu.make_async_remote_copy(
            src_ref=o_part(target),
            dst_ref=o_place,
            send_sem=send_sem.at[O, s],
            recv_sem=recv_sem.at[O, s],
            device_id={"row": target},
            device_id_type=MESH,
        )

    for s in range(1, rows_n):
        o_copy(s).start()
    own_block("o", o_part(my_row), o_place)

    told("second")
    shifted_out("lift")

    each(lambda s: early_copy(s).wait_send())
    for group in LATE:
        each(lambda s, group=group: rs_copy(group, s).wait_send())
        each(lambda s, group=group: ag_copy(group, s).wait_send())
    for copy in own:
        copy.wait()
    for s in range(1, rows_n):
        o_copy(s).wait()
    for p in ROW_SPLIT:
        each(lambda s, p=p: block_copy(p, s).wait())


def write_out(*refs):
    n = len(NAMES)
    copies = [pltpu.make_async_copy(refs[i], refs[n + i], refs[2 * n].at[i]) for i in range(n)]
    for copy in copies:
        copy.start()
    for copy in copies:
        copy.wait()


def solution(mesh):
    def on_device(*args):
        bases = {p: args[4 * i] for i, p in enumerate(NAMES)}
        rank = args[1].shape[0]
        plan = Plan(mesh, bases, rank)
        width, cols_n = plan.width, plan.cols_n
        bf16, f32 = jnp.bfloat16, jnp.float32
        operands, scratch = [], []
        for i, p in enumerate(NAMES):
            base, down, up, magnitude = args[4 * i : 4 * i + 4]
            operands += [base, down, up.T, magnitude]
            scratch += [
                pltpu.VMEM(base.shape, bf16),
                pltpu.VMEM(down.shape, bf16),
                pltpu.VMEM((rank, base.shape[0]), bf16),
                pltpu.VMEM(magnitude.shape, f32),
            ]
        shapes = []
        for p in NAMES:
            if p == "o":
                shapes.append((width // plan.rows_n, plan.height[p] * plan.rows_n))
                scratch.append(pltpu.VMEM((width, plan.height[p]), f32))
            else:
                shapes.append((plan.held[p], width * cols_n))
                scratch.append(pltpu.VMEM((plan.tiles[p] * LANES, width), f32))
        for p in NAMES:
            if p == "o":
                scratch.append(pltpu.VMEM((width, plan.height[p]), bf16))
            else:
                scratch.append(pltpu.VMEM((cols_n, plan.held[p], width), bf16))
        scratch.append(pltpu.VMEM((max(plan.tiles.values()) * LANES, LANES), f32))
        scratch.append(pltpu.VMEM((8, LANES), f32))
        scratch.append(pltpu.VMEM((cols_n, plan.early_rows, LANES), f32))
        scratch += [pltpu.VMEM((cols_n, plan.share[g], LANES), f32) for g in LATE] * 3
        scratch.append(pltpu.VMEM((plan.early_rows, LANES), f32))
        scratch += [
            pltpu.SemaphoreType.DMA((24,)),
            pltpu.SemaphoreType.DMA((6,)),
            pltpu.SemaphoreType.DMA((12, cols_n)),
            pltpu.SemaphoreType.DMA((12, cols_n)),
        ]
        got = pl.pallas_call(
            lambda *refs: kernel(plan, *refs),
            out_shape=[pltpu.VMEM(s, bf16) for s in shapes],
            in_specs=[pl.BlockSpec(memory_space=pl.ANY)] * len(operands),
            out_specs=[pl.BlockSpec(memory_space=pl.ANY)] * len(shapes),
            scratch_shapes=scratch,
            name="merge",
            compiler_params=pltpu.CompilerParams(
                collective_id=0, has_side_effects=True, vmem_limit_bytes=50 * 1024 * 1024
            ),
        )(*operands)
        got = pl.pallas_call(
            write_out,
            out_shape=[jax.ShapeDtypeStruct(s, bf16) for s in shapes],
            in_specs=[pl.BlockSpec(memory_space=pl.ANY)] * len(shapes),
            out_specs=[pl.BlockSpec(memory_space=pl.ANY)] * len(shapes),
            scratch_shapes=[pltpu.SemaphoreType.DMA((len(shapes),))],
            name="write_out",
            compiler_params=pltpu.CompilerParams(vmem_limit_bytes=2 * 1024 * 1024),
        )(*got)
        outs = []
        for p, o in zip(NAMES, got):
            outs.append(o.T if p == "o" else o[: plan.block[p]])
        return tuple(outs)

    specs = []
    for p in NAMES:
        specs += [P("row", "col"), P(None, "col"), P("row", None), P("row")]
    by_row = P(("row", "col"), None)
    return jax.shard_map(
        on_device,
        mesh=mesh,
        in_specs=tuple(specs),
        out_specs=(by_row, by_row, by_row, P(None, ("col", "row")), by_row, by_row),
        check_vma=False,
    )
```

time: 160 us -> 135 us (0.84)
  local copies, waits for them, and re-layouts: 15.8 us -> 0 us
  Pallas kernels: 142 us -> 134 us
    unnamed x10 -> x0, local copies, waits for them, and re-layouts: 13.1 us -> none
    pallas_call x1 -> x2, Pallas kernels: 142 us -> 134 us  [the longest x1 130 us: on_device(): pl.pallas_call(lambda *refs: kernel(plan, *refs), out_shape=[pltpu.VMEM(s...]
    reshape x2 -> x0, local copies, waits for them, and re-layouts: 2.66 us -> none  [on_device(): operands += [base, down, up.T, magnitude.reshape(1, -1)]]
where the time goes in v2:
time: 135 us
  Pallas kernels  134 us (99%)
    pallas_call x1, Pallas kernels, on_device(): pl.pallas_call(lambda *refs: kernel(plan, *refs), out_shape=[pltpu.VMEM(s...  130 us
    pallas_call x1, Pallas kernels, on_device(): pl.pallas_call(write_out, out_shape=[jax.ShapeDtypeStruct(s, bf16) for s...  3.96 us

profile of v2, /device:TPU:1, one launch (start us, length us, event | category | flops | bytes accessed | tf_op | source)
XLA Modules:
  0.0 134.7 jit_solution(11840323523384034006)
XLA Ops:
  0.6 130.1 %merge.1 = (bf16[64,8192]{1,0:T(8,128)(2,1)S(1)}, bf16[8,8192]{1,0:T(8,128)(2,1)S(1)}, bf16[8,8192]{1,0:T(8,128)(2,1)S(1)}, bf16[64,8192]{1,0:T(8,128)(2,1)S(1)}...) custom-call(bf16[1024,512]{1,0:T(8,128)(2,1)} %refs_0_.1, bf16[64,512]{1,0:T(8,128)(2,1)} %refs_1_.1, ...), custom_call_target="tpu_custom_call" | custom-call | tf_op jit(solution)/shard_map/merge/pallas_call | solution.py:448
  130.8 4.0 %write_out.1 = (bf16[64,8192]{1,0:T(8,128)(2,1)}, bf16[8,8192]{1,0:T(8,128)(2,1)}, bf16[8,8192]{1,0:T(8,128)(2,1)}, bf16[64,8192]{1,0:T(8,128)(2,1)}, bf16[232,8...) custom-call(bf16[64,8192]{1,0:T(8,128)(2,1)S(1)} %get-tuple-element.18.refs_0_, ...), custom_call_target="tpu_custom_call" | custom-call | tf_op jit(solution)/shard_map/write_out/pallas_call | solution.py:459
